TPU v7x, 32 devices: a whole 2x2x4 slice. The times are simulated.
32 devices in a mesh: seq: 8 (over z, x), chan: 2 (over y), dp: 2 (over core).
Axes of the slice: x: 2, y: 2, z: 4, core: 2. Of those that a mesh axis runs over, the one named last changes fastest.
Arguments:
- ssm_input: bfloat16 [2, 1024, 4096], P('dp', 'seq', 'chan'), may hold values from -6 to 6
- gate_z: bfloat16 [2, 1024, 4096], P('dp', 'seq', 'chan'), may hold values from -6 to 6
- b_proj: bfloat16 [2, 1024, 128], P('dp', 'seq'), may hold values from -0.52734375 to 0.52734375
- c_proj: bfloat16 [2, 1024, 128], P('dp', 'seq'), may hold values from -6 to 6
- step_size: float32 [2, 1024, 64], P('dp', 'seq', 'chan'), may hold values from 0.02 to 0.2
- log_decay: float32 [2, 1024, 64], P('dp', 'seq', 'chan'), may hold values from -1 to 0, as said below
- skip_d: float32 [64], P('chan'), may hold values from 0.5 to 1.5
- norm_gain: float32 [4096], P('chan'), may hold values from 0.5 to 1.5
- w_out: bfloat16 [4096, 2048], P('chan'), may hold values from -0.09375 to 0.09375
- d_out: bfloat16 [2, 1024, 2048], P('dp', 'seq', 'chan'), may hold values from -6 to 6
- game_lengths: int32 [2, 4], P('dp'), may hold values from 1 to 512, 1024 in all within a row
Outputs:
- out: bfloat16 [2, 1024, 2048], P('dp', 'seq', 'chan')
- grad_x: bfloat16 [2, 1024, 4096], P('dp', 'seq', 'chan')
- grad_gain: float32 [4096], P('chan')
- grad_skip: float32 [64], P('chan')
Inputs may be any that keep to these rules, and one draw needn't show every extreme that they name: `game_lengths`: each row's 4 game lengths sum to 1024, and the longest is exactly 512. `log_decay`: a log decay per position and head.
All inputs are finite; a program needn't handle non-finite values.
Results may differ from a plain program's by a relative error of at most 0.017.
Values may be sent and summed in bfloat16 or wider, within the bound.
A program may use at most 64 MiB of HBM per device.

v0:
```python
import functools

import jax
import jax.numpy as jnp
from jax import lax
from jax.experimental import pallas as pl
from jax.experimental.pallas import tpu as pltpu
from jax.sharding import PartitionSpec as P

NORM_EPS = 1e-05
F32 = jnp.float32
BF16 = jnp.bfloat16
MESH = pl.DeviceIdType.MESH
FWD, BWD = 0, 1


def dot(a, b):
    return lax.dot_general(a, b, (((1,), (0,)), ((), ())), preferred_element_type=F32)


def dot_rows(a, b):
    return lax.dot_general(a, b, (((0,), (0,)), ((), ())), preferred_element_type=F32)


def dot_cols(a, b):
    return lax.dot_general(a, b, (((1,), (1,)), ((), ())), preferred_element_type=F32)


def split(value, terms):
    parts = []
    for _ in range(terms):
        part = value.astype(BF16)
        parts.append(part)
        value = value - part.astype(F32)
    return parts


def kernel(
    sizes,
    x_ref,
    b_ref,
    c_ref,
    dt_ref,
    ld_ref,
    skip_ref,
    gain_ref,
    gl_ref,
    z_hbm,
    w_hbm,
    do_hbm,
    out_ref,
    gx_ref,
    gg_ref,
    gs_ref,
    z_ref,
    w_ref,
    dfull,
    running_ref,
    run_row,
    decay_row,
    decay_peer,
    carry_e,
    tdt_e,
    mix_ref,
    inside_ref,
    act_ref,
    gated_ref,
    normed_ref,
    pulled_ref,
    d_ref,
    own_ref,
    tx1,
    rx1,
    txc,
    rxc,
    tx3,
    state_ref,
    stat_tx,
    stat_rx,
    proj_tx,
    proj_rx,
    proj_own,
    red_tx,
    red_rx,
    load_sem,
    dl_sem,
    do_send,
    do_recv,
    dec_sem,
    s1_send,
    s1_recv,
    sc_send,
    sc_recv,
    s3_send,
    s3_recv,
    st_send,
    st_recv,
    pj_send,
    pj_recv,
    rd_send,
    rd_recv,
):
    n_seq, n_chan, n_dp, heads, games, chunks = sizes
    rows, width = x_ref.shape
    hd = width // heads
    half = width // 2
    cw = half // chunks
    total_width = width * n_chan
    nb = out_ref.shape[1]
    seq = lax.axis_index("seq")
    chan = lax.axis_index("chan")
    dp = lax.axis_index("dp")
    mine = lax.rem(seq, 2)
    partner = {"seq": seq + 1 - 2 * mine}
    place = seq // 2
    last = n_seq // 2 - 1

    steps = []
    hop = 1
    while hop < n_dp:
        steps.append({"dp": dp + hop - 2 * hop * lax.rem(dp // hop, 2)})
        hop *= 2
    steps.append(partner)
    far = [{"seq": lax.rem(seq + 2 * k, n_seq)} for k in range(1, n_seq // 2)]
    chan_peers = [{"chan": lax.rem(chan + off, n_chan)} for off in range(1, n_chan)]
    greet = steps + chan_peers + far
    barrier = pltpu.get_barrier_semaphore()
    for peer in greet:
        pl.semaphore_signal(barrier, inc=1, device_id=peer, device_id_type=MESH)

    loads = [
        pltpu.make_async_copy(z_hbm, z_ref, load_sem.at[0]),
        pltpu.make_async_copy(w_hbm, w_ref, load_sem.at[1]),
        pltpu.make_async_copy(do_hbm, dfull.at[0], dl_sem),
    ]
    loads[2].start()
    loads[0].start()
    loads[1].start()

    def remote(src, dst, ssem, rsem, peer):
        return pltpu.make_async_remote_copy(
            src_ref=src, dst_ref=dst, send_sem=ssem, recv_sem=rsem, device_id=peer, device_id_type=MESH
        )

    row_i = lax.broadcasted_iota(jnp.int32, (rows, rows), 0)
    col_i = lax.broadcasted_iota(jnp.int32, (rows, rows), 1)
    causal = row_i >= col_i
    tri = causal.astype(F32).astype(BF16)
    running = jnp.zeros((rows, heads), F32)
    for part in split(ld_ref[...], 3):
        running = running + dot_cols(tri, part)
    running_ref[...] = running
    run_row[...] = running.T
    base = seq * rows
    count_col = jnp.zeros((rows, 1), jnp.int32)
    count_row = jnp.zeros((1, rows), jnp.int32)
    count_end = jnp.zeros((1, 1), jnp.int32)
    pos_col = base + lax.broadcasted_iota(jnp.int32, (rows, 1), 0)
    pos_row = base + lax.broadcasted_iota(jnp.int32, (1, rows), 1)
    pos_end = base + rows - 1 + lax.broadcasted_iota(jnp.int32, (1, 1), 0)
    begin = jnp.int32(0)
    for g in range(games):
        from_here = (begin >= base).astype(jnp.int32)
        count_col = count_col + (pos_col >= begin).astype(jnp.int32) * from_here
        count_row = count_row + (pos_row >= begin).astype(jnp.int32) * from_here
        count_end = count_end + (pos_end >= begin).astype(jnp.int32) * from_here
        begin = begin + gl_ref[0, g]
    end = running[rows - 1 : rows, :]
    carry = jnp.where(count_col == 0, jnp.exp(running), 0.0)
    tail = jnp.where(count_col == count_end, jnp.exp(end - running), 0.0)
    decay = jnp.where(count_end == 0, jnp.exp(end), 0.0)
    spread = (
        lax.broadcasted_iota(jnp.int32, (heads, width), 1) // hd
        == lax.broadcasted_iota(jnp.int32, (heads, width), 0)
    ).astype(F32).astype(BF16)

    def expand(value, terms):
        total = None
        for part in split(value, terms):
            piece = dot(part, spread)
            total = piece if total is None else total + piece
        return total

    tdt_e[...] = expand(tail * dt_ref[...].T, 2)
    row_pad = jnp.concatenate([decay, skip_ref[...], jnp.zeros((6, heads), F32)], axis=0)
    rows_e = expand(row_pad, 3)
    decay_row[...] = rows_e[0:1, :]
    skip_e = rows_e[1:2, :]

    group = 2 if chunks % 2 == 0 else 1
    groups = chunks // group
    gw = group * cw

    def half_cols(which, g):
        return pl.ds(pl.multiple_of(which * half + g * gw, gw), gw)

    def my_cols(c):
        return pl.ds(pl.multiple_of(mine * half + c * cw, cw), cw)

    def send1(d, c):
        return remote(tx1.at[d, c], rx1.at[d, c], s1_send.at[d, c], s1_recv.at[d, c], partner)

    def send3(d, c):
        return remote(
            tx3.at[d, c], state_ref.at[d, mine * chunks + c], s3_send.at[d, c], s3_recv.at[d, c], partner
        )

    def sendc(d, c):
        to = lax.rem(seq + (2 if d == FWD else n_seq - 2), n_seq)
        return remote(txc.at[d, c], rxc.at[d, c], sc_send.at[d, c], sc_recv.at[d, c], {"seq": to})

    has = (place > 0, place < last)
    dec = remote(decay_row, decay_peer, dec_sem.at[0], dec_sem.at[1], partner)

    def make(d, left, value_of):
        for g in range(groups):
            block = dot(left, value_of(half_cols(1 - mine, g))).astype(BF16)
            for k in range(group):
                tx1[d, g * group + k] = block[:, k * cw : (k + 1) * cw]
                send1(d, g * group + k).start()
        for g in range(groups):
            block = dot(left, value_of(half_cols(mine, g)))
            for k in range(group):
                own_ref[g * group + k] = block[:, k * cw : (k + 1) * cw]

    def chain(d):
        first = mine == (0 if d == FWD else 1)
        prev, nxt = (has[0], has[1]) if d == FWD else (has[1], has[0])

        def body(c):
            send1(d, c).wait_recv()

            @pl.when(prev)
            def _():
                sendc(d, c).wait_recv()

            @pl.when(jnp.logical_not(prev))
            def _():
                rxc[d, c] = jnp.zeros((rxc.shape[2], cw), BF16)

            dec_me = decay_row[:, my_cols(c)]
            dec_peer = decay_peer[:, my_cols(c)]
            fresh = own_ref[c]
            fresh_peer = rx1[d, c].astype(F32)
            before = rxc[d, c].astype(F32)
            after_me = dec_me * before + fresh
            after_peer = dec_peer * before + fresh_peer

            @pl.when(nxt)
            def _():
                txc[d, c] = jnp.where(
                    first, dec_peer * after_me + fresh_peer, dec_me * after_peer + fresh
                ).astype(BF16)
                sendc(d, c).start()

            tx3[d, c] = jnp.where(first, after_me, before).astype(BF16)

            @pl.when(prev)
            def _():
                send3(d, c).start()

            state_ref[d, mine * chunks + c] = jnp.where(first, before, after_peer).astype(BF16)

        for c in range(chunks):
            body(c)

    def head_sends(d):
        for c in range(chunks):
            send3(d, c).start()

    pl.semaphore_wait(barrier, len(greet))
    dec.start()
    loads[2].wait()
    do_copies = []
    for k, peer in enumerate(chan_peers):
        do_copies.append(remote(dfull.at[0], dfull.at[k + 1], do_send.at[k], do_recv.at[k], peer))
        do_copies[-1].start()
    b_t = b_ref[...].T
    make(FWD, b_t, lambda cols: (tdt_e[:, cols] * x_ref[:, cols].astype(F32)).astype(BF16))

    scores = jnp.where(causal & (count_col == count_row), dot_cols(c_ref[...], b_ref[...]), 0.0)
    pos_lane = lax.broadcasted_iota(jnp.int32, (rows, 2 * hd), 1) < hd
    carry_e[...] = expand(carry, 2)
    loads[0].wait()

    def block_diag(pair):
        pair = pair.astype(F32)
        return jnp.concatenate(
            [jnp.where(pos_lane, pair, 0.0), jnp.where(pos_lane, 0.0, pair)], axis=0
        ).astype(BF16)

    for q in range(heads // 2):
        cols = slice(q * 2 * hd, (q + 1) * 2 * hd)
        mixes = []
        for h in (2 * q, 2 * q + 1):
            gap = jnp.minimum(running_ref[:, h : h + 1] - run_row[h : h + 1, :], 0.0)
            mixes.append((jnp.exp(gap) * scores * dt_ref[h : h + 1, :]).astype(BF16))
            mix_ref[q, (h % 2) * rows : (h % 2 + 1) * rows, :] = mixes[-1]
        pair = x_ref[:, cols]
        inside_ref[:, cols] = dot(jnp.concatenate(mixes, axis=1), block_diag(pair)) + skip_e[
            :, cols
        ] * pair.astype(F32)
        zf = z_ref[:, cols].astype(F32)
        act_ref[:, cols] = zf / (1.0 + jnp.exp(-zf))

    tile = min(256, width)

    def pull():
        loads[1].wait()
        for copy in do_copies:
            copy.wait_recv()

        def body(i, _):
            feats = pl.ds(pl.multiple_of(i * tile, tile), tile)
            total = None
            for k in range(n_chan):
                source = lax.rem(chan + n_chan - k, n_chan)
                piece = dot_cols(dfull[k], w_ref[feats, pl.ds(pl.multiple_of(source * nb, nb), nb)])
                total = piece if total is None else total + piece
            pulled_ref[:, feats] = total
            return 0

        lax.fori_loop(0, width // tile, body, 0)

    pl.when(place == last)(pull)
    dec.wait_recv()
    chain(FWD)
    pl.when(place == 0)(lambda: head_sends(FWD))
    pl.when(place < last)(pull)

    def gate(q, sums):
        squares, dots = sums
        cols = pl.ds(pl.multiple_of(q * gw, gw), gw)
        carried = jnp.concatenate(
            [dot(c_ref[...], state_ref[FWD, q * group + k]) for k in range(group)], axis=1
        )
        gated = (inside_ref[:, cols] + carry_e[:, cols] * carried) * act_ref[:, cols]
        normed = (gated * gain_ref[:, cols]).astype(BF16)
        gated_ref[:, cols] = gated
        normed_ref[:, cols] = normed
        sq = gated * gated
        od = normed.astype(F32) * pulled_ref[:, cols]
        for k in range(gw // 128):
            squares = squares + sq[:, k * 128 : (k + 1) * 128]
            dots = dots + od[:, k * 128 : (k + 1) * 128]
        return squares, dots

    zero = jnp.zeros((rows, 128), F32)
    sums = lax.fori_loop(0, groups, lambda g, s: gate(mine * groups + g, s), (zero, zero))

    def gate_late(d):
        def body(g, s):
            for k in range(group):
                send3(d, g * group + k).wait_recv()
            return gate((1 - mine) * groups + g, s)

        return body

    squares, dots = lax.fori_loop(0, groups, gate_late(FWD), sums)
    sq_col = jnp.sum(squares, axis=1, keepdims=True)
    dot_col = jnp.sum(dots, axis=1, keepdims=True)
    lane = lax.broadcasted_iota(jnp.int32, (rows, 128), 1)
    stats = jnp.where(lane == 0, sq_col, jnp.where(lane == 1, dot_col, 0.0))
    stat_tx[...] = stats.T[0:8, :]
    st_copies = []
    for k, peer in enumerate(chan_peers):
        st_copies.append(remote(stat_tx, stat_rx.at[k], st_send.at[k], st_recv.at[k], peer))
        st_copies[-1].start()
    total = stat_tx[...]
    for k, copy in enumerate(st_copies):
        copy.wait_recv()
        total = total + stat_rx[k]
    stat_cols = jnp.concatenate([total, jnp.zeros((rows - 8, rows), F32)], axis=0).T
    inv = lax.rsqrt(stat_cols[:, 0:1] / total_width + NORM_EPS)
    back = inv * inv * inv * stat_cols[:, 1:2] / total_width

    c_t = c_ref[...].T

    def cot_block(cols):
        gated = gated_ref[:, cols]
        d_normed = inv * pulled_ref[:, cols]
        d = ((gain_ref[:, cols] * d_normed - back * gated) * act_ref[:, cols]).astype(BF16)
        d_ref[:, cols] = d
        pulled_ref[:, cols] = gated * d_normed
        return (carry_e[:, cols] * d.astype(F32)).astype(BF16)

    make(BWD, c_t, cot_block)

    def cot(q, _):
        cols = pl.ds(pl.multiple_of(q * gw, gw), gw)
        red_tx[0, 0:1, cols] = jnp.sum(pulled_ref[:, cols], axis=0, keepdims=True)
        red_tx[0, 1:2, cols] = jnp.sum(
            d_ref[:, cols].astype(F32) * x_ref[:, cols].astype(F32), axis=0, keepdims=True
        )
        return 0

    lax.fori_loop(0, 2 * groups, cot, 0)

    def red(k):
        return remote(red_tx.at[k], red_rx.at[k], rd_send.at[k], rd_recv.at[k], steps[k])

    def reduce_step(k):
        red(k).wait_recv()
        red_tx[k + 1] = red_tx[k] + red_rx[k]
        if k + 1 < len(steps):
            red(k + 1).start()

    def red_far(k):
        slot = len(steps) + k
        return remote(red_tx.at[len(steps)], red_rx.at[slot], rd_send.at[slot], rd_recv.at[slot], far[k])

    red(0).start()
    tile_n = min(256, nb)

    def project(block, store):
        def body(i, _):
            at = pl.ds(pl.multiple_of(block * nb + i * tile_n, tile_n), tile_n)
            store(pl.ds(pl.multiple_of(i * tile_n, tile_n), tile_n), dot(normed_ref[...], w_ref[:, at]))
            return 0

        lax.fori_loop(0, nb // tile_n, body, 0)

    pj_copies = []
    for k, peer in enumerate(chan_peers):

        def store(at, value, k=k):
            proj_tx[k, :, at] = value.astype(BF16)

        project(peer["chan"], store)
        pj_copies.append(remote(proj_tx.at[k], proj_rx.at[k], pj_send.at[k], pj_recv.at[k], peer))
        pj_copies[-1].start()

    pl.when(place == last)(lambda: chain(BWD))
    reduce_step(0)
    def own_body(i, _):
        at = pl.ds(pl.multiple_of(chan * nb + i * tile_n, tile_n), tile_n)
        proj_own[:, pl.ds(pl.multiple_of(i * tile_n, tile_n), tile_n)] = dot(normed_ref[...], w_ref[:, at])
        return 0

    lax.fori_loop(0, nb // tile_n, own_body, 0)
    for q in range(heads // 2):
        cols = slice(q * 2 * hd, (q + 1) * 2 * hd)
        pair = d_ref[:, cols]
        inside_ref[:, cols] = dot_rows(mix_ref[q], block_diag(pair)) + skip_e[:, cols] * pair.astype(F32)

    def finish_out():
        for copy in pj_copies:
            copy.wait_recv()
        for i in range(nb // tile_n):
            at = slice(i * tile_n, (i + 1) * tile_n)
            value = proj_own[:, at]
            for k in range(n_chan - 1):
                value = value + proj_rx[k, :, at].astype(F32)
            out_ref[:, at] = (inv * value).astype(BF16)

    def settle():
        for k in range(1, len(steps)):
            reduce_step(k)
        for k in range(len(far)):
            red_far(k).start()
        finish_out()

    pl.when(place < last - 1)(settle)
    pl.when(place < last)(lambda: chain(BWD))
    pl.when(place >= last - 1)(settle)
    pl.when(place == last)(lambda: head_sends(BWD))

    def finish(q):
        cols = pl.ds(pl.multiple_of(q * gw, gw), gw)
        carried = jnp.concatenate(
            [dot(b_ref[...], state_ref[BWD, q * group + k]) for k in range(group)], axis=1
        )
        gx_ref[:, cols] = (inside_ref[:, cols] + tdt_e[:, cols] * carried).astype(BF16)

    def early(g, _):
        finish(mine * groups + g)
        return 0

    def late(g, _):
        for k in range(group):
            send3(BWD, g * group + k).wait_recv()
        finish((1 - mine) * groups + g)
        return 0

    lax.fori_loop(0, groups, early, 0)
    lax.fori_loop(0, groups, late, 0)

    final = red_tx[len(steps)]
    for k in range(len(far)):
        red_far(k).wait_recv()
        final = final + red_rx[len(steps) + k]
    gg_ref[...] = final[0:1, :]
    skip_cols = jnp.concatenate([final[1:2, :], jnp.zeros((7, width), F32)], axis=0)
    skip_sum = jnp.zeros((8, heads), F32)
    for part in split(skip_cols, 3):
        skip_sum = skip_sum + dot_cols(part, spread)
    gs_ref[...] = skip_sum[0:1, :]

    dec.wait_send()
    for copy in do_copies + st_copies + pj_copies:
        copy.wait_send()
    for k in range(len(steps)):
        red(k).wait_send()
    for k in range(len(far)):
        red_far(k).wait_send()
    for d in (FWD, BWD):
        for c in range(chunks):
            send1(d, c).wait_send()
            send3(d, c).wait_send()

            @pl.when(has[1] if d == FWD else has[0])
            def _():
                sendc(d, c).wait_send()


def hand_over(*refs):
    for source, target in zip(refs[:4], refs[4:]):
        target[...] = source[...]


def local(
    mesh_shape, ssm_input, gate_z, b_proj, c_proj, step_size, log_decay, skip_d, norm_gain, w_out, d_out, game_lengths
):
    n_seq, n_chan, n_dp = (mesh_shape[a] for a in ("seq", "chan", "dp"))
    _, rows, width = ssm_input.shape
    heads = step_size.shape[2]
    states = b_proj.shape[2]
    model = w_out.shape[1]
    nb = d_out.shape[2]
    half = width // 2
    chunks = max(1, min(8, half // 128))
    cw = half // chunks
    reds = n_dp.bit_length()
    slots = reds + n_seq // 2 - 1
    peers = max(1, n_chan - 1)
    sizes = (n_seq, n_chan, n_dp, heads, game_lengths.shape[1], chunks)
    vmem = pl.BlockSpec(memory_space=pltpu.VMEM)
    hbm = pl.BlockSpec(memory_space=pltpu.HBM)
    dma = pltpu.SemaphoreType.DMA
    out, gx, gg, gs = pl.pallas_call(
        functools.partial(kernel, sizes),
        out_shape=(
            pltpu.VMEM((rows, nb), BF16),
            pltpu.VMEM((rows, width), BF16),
            pltpu.VMEM((1, width), F32),
            pltpu.VMEM((1, heads), F32),
        ),
        in_specs=[vmem] * 7 + [pl.BlockSpec(memory_space=pltpu.SMEM)] + [hbm] * 3,
        out_specs=(vmem,) * 4,
        scratch_shapes=[
            pltpu.VMEM((rows, width), BF16),
            pltpu.VMEM((width, model), BF16),
            pltpu.VMEM((n_chan, rows, nb), BF16),
            pltpu.VMEM((rows, heads), F32),
            pltpu.VMEM((heads, rows), F32),
            pltpu.VMEM((1, width), F32),
            pltpu.VMEM((1, width), F32),
            pltpu.VMEM((rows, width), F32),
            pltpu.VMEM((rows, width), F32),
            pltpu.VMEM((heads // 2, 2 * rows, rows), BF16),
            pltpu.VMEM((rows, width), F32),
            pltpu.VMEM((rows, width), F32),
            pltpu.VMEM((rows, width), F32),
            pltpu.VMEM((rows, width), BF16),
            pltpu.VMEM((rows, width), F32),
            pltpu.VMEM((rows, width), BF16),
            pltpu.VMEM((chunks, states, cw), F32),
            pltpu.VMEM((2, chunks, states, cw), BF16),
            pltpu.VMEM((2, chunks, states, cw), BF16),
            pltpu.VMEM((2, chunks, states, cw), BF16),
            pltpu.VMEM((2, chunks, states, cw), BF16),
            pltpu.VMEM((2, chunks, states, cw), BF16),
            pltpu.VMEM((2, 2 * chunks, states, cw), BF16),
            pltpu.VMEM((8, rows), F32),
            pltpu.VMEM((peers, 8, rows), F32),
            pltpu.VMEM((peers, rows, nb), BF16),
            pltpu.VMEM((peers, rows, nb), BF16),
            pltpu.VMEM((rows, nb), F32),
            pltpu.VMEM((reds + 1, 2, width), F32),
            pltpu.VMEM((slots, 2, width), F32),
            dma((2,)),
            dma,
            dma((peers,)),
            dma((peers,)),
            dma((2,)),
            dma((2, chunks)),
            dma((2, chunks)),
            dma((2, chunks)),
            dma((2, chunks)),
            dma((2, chunks)),
            dma((2, chunks)),
            dma((peers,)),
            dma((peers,)),
            dma((peers,)),
            dma((peers,)),
            dma((slots,)),
            dma((slots,)),
        ],
        compiler_params=pltpu.CompilerParams(
            collective_id=0, has_side_effects=True, vmem_limit_bytes=60 * 1024 * 1024
        ),
    )(
        ssm_input[0],
        b_proj[0],
        c_proj[0],
        step_size[0].T,
        log_decay[0].T,
        skip_d[None],
        norm_gain[None],
        game_lengths,
        gate_z[0],
        w_out,
        d_out[0],
    )
    results = (out, gx, gg, gs)
    out, gx, gg, gs = pl.pallas_call(
        hand_over,
        out_shape=tuple(jax.ShapeDtypeStruct(a.shape, a.dtype) for a in results),
        in_specs=[vmem] * 4,
        out_specs=(vmem,) * 4,
        compiler_params=pltpu.CompilerParams(vmem_limit_bytes=4 * 1024 * 1024),
    )(*results)
    return out[None], gx[None], gg[0], gs[0]


def solution(mesh):
    return jax.shard_map(
        functools.partial(local, dict(mesh.shape)),
        mesh=mesh,
        in_specs=(
            P("dp", "seq", "chan"),
            P("dp", "seq", "chan"),
            P("dp", "seq", None),
            P("dp", "seq", None),
            P("dp", "seq", "chan"),
            P("dp", "seq", "chan"),
            P("chan"),
            P("chan"),
            P("chan", None),
            P("dp", "seq", "chan"),
            P("dp", None),
        ),
        out_specs=(P("dp", "seq", "chan"), P("dp", "seq", "chan"), P("chan"), P("chan")),
        check_vma=False,
    )
```

profile of v0, /device:TPU:0, one launch (start us, length us, event | category | flops | bytes accessed | tf_op | source)
XLA Modules:
  0.0 50.5 jit_solution(4425249286192740878)
XLA Ops:
  0.6 48.9 %shard_map.138 = (bf16[128,1024]{1,0:T(8,128)(2,1)S(1)}, bf16[128,2048]{1,0:T(8,128)(2,1)S(1)}, f32[1,2048]{1,0:T(1,128)S(1)}, f32[1,32]{1,0:T(1,128)S(1)}) custom-call(bf16[128,2048]{1,0:T(8,128)(2,1)} %bitcast.17, bf16[128,128]{1,0:T(8,128)(2,1)} %bitcast.20, bf16[128,128]{1,0:T(8,128)(2,1)} %bitcast.21, f32[32,128]{1,0:T(8,128)} %bitcast.22, ...), custom_call_target="tpu_custom_call" | custom-call | tf_op jit(solution)/shard_map/pallas_call | solution.py:540
  49.5 0.9 %shard_map.139 = (bf16[128,1024]{1,0:T(8,128)(2,1)}, bf16[128,2048]{1,0:T(8,128)(2,1)}, f32[1,2048]{1,0:T(1,128)}, f32[1,32]{1,0:T(1,128)}) custom-call(bf16[128,1024]{1,0:T(8,128)(2,1)S(1)} %get-tuple-element.12.refs_0_, bf16[128,2048]{1,0:T(8,128)(2,1)S(1)} %get-tuple-element.13.refs_1_, f32[1,2048]{1,0:T(1,128)S(1)} %get-tuple-element.14.refs_2_, ...), custom_call_target="tpu_custom_call" | custom-call | tf_op jit(solution)/shard_map/pallas_call | solution.py:616
where the time goes:
time: 50.6 us; the launch traced here: 50.5 us
  Pallas kernels  49.8 us (98%)
  between operations  0.64 us (1%)
    pallas_call x1, Pallas kernels, local(): pl.pallas_call(functools.partial(kernel, sizes), out_shape=(pltpu.VMEM((r...  48.9 us

commit v1 on v0

v1 whole, which is shorter than its diff:
```python
import functools
import types

import jax
import jax.numpy as jnp
from jax import lax
from jax.experimental import pallas as pl
from jax.experimental.pallas import tpu as pltpu
from jax.sharding import PartitionSpec as P

NORM_EPS = 1e-05
F32 = jnp.float32
BF16 = jnp.bfloat16
MESH = pl.DeviceIdType.MESH
FWD, BWD = 0, 1


def dot(a, b):
    return lax.dot_general(a, b, (((1,), (0,)), ((), ())), preferred_element_type=F32)


def dot_rows(a, b):
    return lax.dot_general(a, b, (((0,), (0,)), ((), ())), preferred_element_type=F32)


def dot_cols(a, b):
    return lax.dot_general(a, b, (((1,), (1,)), ((), ())), preferred_element_type=F32)


def split(value, terms):
    parts = []
    for _ in range(terms):
        part = value.astype(BF16)
        parts.append(part)
        value = value - part.astype(F32)
    return parts


def kernel(sizes, names, *refs):
    r = types.SimpleNamespace(**dict(zip(names, refs)))
    n_seq, n_chan, n_dp, heads, games, chunks, group = sizes
    rows, width = r.x.shape
    hd = width // heads
    half = width // 2
    hh = heads // 2
    cw = half // chunks
    gw = group * cw
    groups = chunks // group
    total_width = width * n_chan
    nb = r.out.shape[1]
    seq = lax.axis_index("seq")
    chan = lax.axis_index("chan")
    dp = lax.axis_index("dp")
    mine = lax.rem(seq, 2)
    other = 1 - mine
    pair = seq + 1 - 2 * mine
    partner = {"seq": pair}
    place = seq // 2
    last = n_seq // 2 - 1
    has_prev, has_next = place > 0, place < last
    prev_dev = {"seq": lax.rem(seq + n_seq - 2, n_seq)}
    next_dev = {"seq": lax.rem(seq + 2, n_seq)}

    siblings = [{"dp": lax.rem(dp + k, n_dp)} for k in range(1, n_dp)]
    offs = [lax.rem(chan + off, n_chan) for off in range(1, n_chan)]
    chan_peers = [{"chan": o} for o in offs]
    stat_peers = [partner] + chan_peers + [{"seq": pair, "chan": o} for o in offs]
    greet = [partner] + chan_peers + siblings
    barrier = pltpu.get_barrier_semaphore()

    def hello(peer):
        pl.semaphore_signal(barrier, inc=1, device_id=peer, device_id_type=MESH)

    for peer in greet:
        hello(peer)
    pl.when(has_prev)(lambda: hello(prev_dev))
    pl.when(has_next)(lambda: hello(next_dev))

    my_half = pl.ds(pl.multiple_of(mine * half, half), half)
    other_half = pl.ds(pl.multiple_of(other * half, half), half)
    order = {}

    def load(name, src, dst):
        order[name] = pltpu.make_async_copy(src, dst, r.load_sem.at[len(order)])
        order[name].start()

    def load_chunks(name, which, dst):
        for c in range(chunks):
            at = pl.ds(pl.multiple_of(which * half + c * cw, cw), cw)
            pltpu.make_async_copy(r.x.at[:, at], dst.at[c], r.load_sem.at[len(order)]).start()
        order[name] = pltpu.make_async_copy(dst, dst, r.load_sem.at[len(order)])

    load("ld", r.ld, r.ldv)
    load("gl", r.gl, r.gls)
    load("dt", r.dt, r.smf.at[1])
    load("b", r.b, r.bv.at[mine])
    load_chunks("xo", other, r.xo)
    load("do", r.do, r.dfull.at[0])
    load_chunks("x", mine, r.xv.at[mine])
    load("c", r.c, r.cv.at[mine])
    load("skip", r.skip, r.skipv)
    load("zo", r.z.at[:, other_half], r.zo)
    load("z", r.z.at[:, my_half], r.zv.at[mine])
    load("gain", r.gain, r.gainv)
    load("w", r.w, r.wv)

    def remote(src, dst, ssem, rsem, peer):
        return pltpu.make_async_remote_copy(
            src_ref=src, dst_ref=dst, send_sem=ssem, recv_sem=rsem, device_id=peer, device_id_type=MESH
        )

    def ccols(c):
        return pl.ds(pl.multiple_of(c * cw, cw), cw)

    def gcols(g):
        return pl.ds(pl.multiple_of(g * gw, gw), gw)

    def gain_of(g):
        return r.gainv[:, pl.ds(pl.multiple_of(mine * half + g * gw, gw), gw)]

    def send_sm(blk):
        src = r.smf.at[:, pl.ds(pl.multiple_of(other * hh, hh), hh), :]
        return remote(src, r.sm.at[blk], r.p_send.at[0], r.p_recv.at[0], partner)

    def send_b(blk):
        return remote(r.bv.at[blk], r.bv.at[blk], r.p_send.at[1], r.p_recv.at[1], partner)

    def send_c(blk):
        return remote(r.cv.at[blk], r.cv.at[blk], r.p_send.at[2], r.p_recv.at[2], partner)

    def send_z(blk):
        return remote(r.zo, r.zv.at[blk], r.p_send.at[3], r.p_recv.at[3], partner)

    def send_n():
        return remote(r.nrm.at[other], r.nrx, r.p_send.at[4], r.p_recv.at[4], partner)

    def send_x(blk, c):
        return remote(r.xo.at[c], r.xv.at[blk, c], r.x_send, r.x_recv.at[c], partner)

    def send_p(blk, g):
        return remote(r.ptx.at[g], r.pv.at[blk, g], r.pl_send, r.pl_recv.at[g], partner)

    def send_g(c, of):
        at = pl.ds(pl.multiple_of(of * half + c * cw, cw), cw)
        return remote(r.gtx.at[c], r.gx.at[:, at], r.g_send, r.g_recv.at[c], partner)

    def send_chain(d, c):
        to = next_dev if d == FWD else prev_dev
        return remote(r.txc.at[d, c], r.st.at[d, d, c], r.c_send.at[d], r.c_recv.at[d, c], to)

    do_copies = [
        remote(r.dfull.at[0], r.dfull.at[k + 1], r.do_send.at[k], r.do_recv.at[k], peer)
        for k, peer in enumerate(chan_peers)
    ]

    row_i = lax.broadcasted_iota(jnp.int32, (rows, rows), 0)
    col_i = lax.broadcasted_iota(jnp.int32, (rows, rows), 1)
    causal = row_i >= col_i
    tri = causal.astype(F32).astype(BF16)
    spread = (
        lax.broadcasted_iota(jnp.int32, (hh, half), 1) // hd == lax.broadcasted_iota(jnp.int32, (hh, half), 0)
    ).astype(F32).astype(BF16)

    def spread_all(which):
        at = lax.broadcasted_iota(jnp.int32, (heads, half), 1) // hd + which * hh
        return (at == lax.broadcasted_iota(jnp.int32, (heads, half), 0)).astype(F32).astype(BF16)

    order["ld"].wait()
    running = jnp.zeros((heads, rows), F32)
    for part in split(r.ldv[...], 3):
        running = running + dot_cols(part, tri)
    r.smf[0] = running
    order["gl"].wait()

    def counts(blk):
        base = (2 * place + blk) * rows
        col = jnp.zeros((rows, 1), jnp.int32)
        row = jnp.zeros((1, rows), jnp.int32)
        end = jnp.zeros((1, 1), jnp.int32)
        pos_col = base + lax.broadcasted_iota(jnp.int32, (rows, 1), 0)
        pos_row = base + lax.broadcasted_iota(jnp.int32, (1, rows), 1)
        pos_end = base + rows - 1 + lax.broadcasted_iota(jnp.int32, (1, 1), 0)
        begin = jnp.int32(0)
        for g in range(games):
            here = (begin >= base).astype(jnp.int32)
            col = col + (pos_col >= begin).astype(jnp.int32) * here
            row = row + (pos_row >= begin).astype(jnp.int32) * here
            end = end + (pos_end >= begin).astype(jnp.int32) * here
            begin = begin + r.gls[0, g]
        return col, row, end

    def expand(value, terms):
        total = None
        for part in split(value, terms):
            piece = dot_rows(part, spread)
            total = piece if total is None else total + piece
        return total

    def prepare(blk):
        run = r.sm[blk, 0]
        _, row, end = counts(blk)
        carry = jnp.where(row == 0, jnp.exp(run), 0.0)
        tail = jnp.where(row == end, jnp.exp(run[:, rows - 1 : rows] - run), 0.0)
        r.tdt_e[blk] = expand(tail * r.sm[blk, 1], 2)
        r.carry_e[blk] = expand(carry, 2)
        r.runc[blk] = run.T
        r.bt[blk] = r.bv[blk].T

    my_heads = pl.ds(pl.multiple_of(mine * hh, hh), hh)
    order["dt"].wait()
    r.sm[mine] = r.smf[:, my_heads, :]
    order["b"].wait()
    prepare(mine)

    def report():
        pl.semaphore_signal(r.up, inc=1, device_id=prev_dev, device_id_type=MESH)

    def relay():
        pl.semaphore_wait(r.up, 1)
        pl.when(has_prev)(report)

    static = len(greet)
    pl.semaphore_wait(barrier, static + has_prev.astype(jnp.int32) + has_next.astype(jnp.int32))
    pl.when(place == last)(report)
    order["xo"].wait()
    order["do"].wait()
    order["c"].wait()
    order["zo"].wait()

    def first_sends():
        send_sm(mine).start()
        send_b(mine).start()
        for c in range(chunks):
            send_x(mine, c).start()
        send_c(mine).start()

    def cotangent_sends():
        for copy in do_copies:
            copy.start()

    def lead_sends():
        first_sends()
        cotangent_sends()

    def gate_sends():
        send_z(mine).start()

    pl.when(dp == 0)(lead_sends)
    pl.when((dp == 0) & (place >= last - 1))(gate_sends)
    order["x"].wait()

    def x_group(blk, g):
        return jnp.concatenate([r.xv[blk, g * group + k] for k in range(group)], axis=1).astype(F32)


    def fresh(blk, g):
        cols = gcols(g)
        scaled = (r.tdt_e[blk, :, cols] * x_group(blk, g)).astype(BF16)
        block = dot(r.bt[blk], scaled)
        for k in range(group):
            r.f[blk, g * group + k] = block[:, k * cw : (k + 1) * cw]

    def loop(n, body):
        def step(i, _):
            body(i)
            return 0

        lax.fori_loop(0, n, step, 0)

    loop(groups, lambda g: fresh(mine, g))
    order["skip"].wait()
    skip_pad = jnp.concatenate([r.skipv[...], jnp.zeros((7, heads), F32)], axis=0)
    skip_rows = None
    for part in split(skip_pad, 3):
        piece = dot(part, spread_all(mine))
        skip_rows = piece if skip_rows is None else skip_rows + piece
    r.skip_e[...] = skip_rows[0:1, :]
    pos_lane = lax.broadcasted_iota(jnp.int32, (rows, 2 * hd), 1) < hd

    def block_diag(two):
        two = two.astype(F32)
        return jnp.concatenate(
            [jnp.where(pos_lane, two, 0.0), jnp.where(pos_lane, 0.0, two)], axis=0
        ).astype(BF16)

    def intra(blk):
        col, row, _ = counts(blk)
        r.ct[blk] = r.cv[blk].T
        scores = jnp.where(causal & (col == row), dot_cols(r.cv[blk], r.bv[blk]), 0.0)
        for q in range(hh // 2):
            cols = slice(q * 2 * hd, (q + 1) * 2 * hd)
            mixes = []
            for h in (2 * q, 2 * q + 1):
                gap = jnp.minimum(r.runc[blk, :, h : h + 1] - r.sm[blk, 0, h : h + 1, :], 0.0)
                mixes.append((jnp.exp(gap) * scores * r.sm[blk, 1, h : h + 1, :]).astype(BF16))
                r.mix[blk, q, (h % 2) * rows : (h % 2 + 1) * rows, :] = mixes[-1]
            at = q * 2 * hd
            two = r.xv[blk, at // cw, :, at % cw : at % cw + 2 * hd]
            r.inside[blk, :, cols] = dot(jnp.concatenate(mixes, axis=1), block_diag(two)) + r.skip_e[
                :, cols
            ] * two.astype(F32)

    def silu(blk):
        def body(g):
            zf = r.zv[blk, :, gcols(g)].astype(F32)
            r.act[blk, :, gcols(g)] = zf / (1.0 + jnp.exp(-zf))

        loop(groups, body)

    def chain(d, c):
        enters = has_prev if d == FWD else has_next
        leaves = has_next if d == FWD else has_prev

        @pl.when(enters)
        def _():
            send_chain(d, c).wait_recv()

        @pl.when(jnp.logical_not(enters))
        def _():
            r.st[d, d, c] = jnp.zeros((r.st.shape[3], cw), BF16)

        one, two = (0, 1) if d == FWD else (1, 0)
        mid = r.carry_e[one, rows - 1 : rows, ccols(c)] * r.st[d, d, c].astype(F32) + r.f[one, c]
        r.st[d, 1 - d, c] = mid.astype(BF16)

        @pl.when(leaves)
        def _():
            r.txc[d, c] = (r.carry_e[two, rows - 1 : rows, ccols(c)] * mid + r.f[two, c]).astype(BF16)
            send_chain(d, c).start()

    def meet(g):
        for k in range(group):
            send_x(other, g * group + k).wait_recv()
        fresh(other, g)

    def partner_arrives():
        send_sm(other).wait_recv()
        send_b(other).wait_recv()

    def chain_group(d, g):
        for k in range(group):
            chain(d, g * group + k)

    def meet_chain(g):
        meet(g)
        chain_group(FWD, g)

    def own_local():
        intra(mine)
        order["z"].wait()
        silu(mine)

    def late_sends():
        own_local()
        pl.semaphore_wait(r.go, 1)
        lead_sends()
        pl.when(place >= last - 1)(gate_sends)

    def lead_done():
        for k in range(1, n_dp):
            pl.semaphore_signal(r.go, inc=1, device_id={"dp": k}, device_id_type=MESH)

    pl.when(dp > 0)(late_sends)
    partner_arrives()
    pl.when((dp == 0) & (place < last - 1))(lead_done)
    prepare(other)
    pl.when(place == last - 1)(relay)

    def pull(lo, hi):
        def body(i, _):
            which = jnp.where(i < groups, other, mine)
            g = lax.rem(i, groups)
            feats = pl.ds(pl.multiple_of(which * half + g * gw, gw), gw)
            total = None
            for k in range(n_chan):
                source = lax.rem(chan + n_chan - k, n_chan)
                piece = dot_cols(r.dfull[k], r.wv[feats, pl.ds(pl.multiple_of(source * nb, nb), nb)])
                total = piece if total is None else total + piece
            value = total.astype(BF16)

            @pl.when(i < groups)
            def _():
                r.ptx[g] = value
                send_p(mine, g).start()

            @pl.when(i >= groups)
            def _():
                r.pv[mine, g] = value

            return 0

        lax.fori_loop(lo, hi, body, 0)

    def pull_ready():
        order["w"].wait()
        for copy in do_copies:
            copy.wait_recv()

    tiles = 2 * groups
    late_place = place >= last - 1

    def pull_first():
        pl.when(dp == 0)(own_local)
        pull_ready()
        pull(0, groups)
        pl.when(dp == 0)(lead_done)

    pl.when(late_place)(pull_first)
    pl.when(place == 0)(lambda: loop(groups, meet_chain))
    pl.when(place > 0)(lambda: loop(groups, meet))
    pl.when((place > 0) & (place < last - 1))(relay)
    pl.when((dp == 0) & (place < last - 1))(own_local)
    send_c(other).wait_recv()
    intra(other)
    pl.when(place < last - 1)(gate_sends)
    pl.when(place == last)(lambda: pull(groups, tiles))
    order["gain"].wait()
    r.sums[...] = jnp.zeros(r.sums.shape, F32)

    def gate(g):
        cols = gcols(g)
        send_p(other, g).wait_recv()
        for blk in (0, 1):
            carried = jnp.concatenate(
                [dot(r.cv[blk], r.st[FWD, blk, g * group + k]) for k in range(group)], axis=1
            )
            gated = (r.inside[blk, :, cols] + r.carry_e[blk, :, cols] * carried) * r.act[blk, :, cols]
            normed = (gated * gain_of(g)).astype(BF16)
            r.gated[blk, :, cols] = gated
            r.nrm[blk, :, cols] = normed
            sq = gated * gated
            od = normed.astype(F32) * r.pv[blk, g].astype(F32)
            squares, dots = r.sums[blk, 0], r.sums[blk, 1]
            for k in range(gw // 128):
                squares = squares + sq[:, k * 128 : (k + 1) * 128]
                dots = dots + od[:, k * 128 : (k + 1) * 128]
            r.sums[blk, 0] = squares
            r.sums[blk, 1] = dots

    def gate_ready():
        send_z(other).wait_recv()
        silu(other)

    def chain_gate(g):
        chain_group(FWD, g)
        gate(g)

    def at_last():
        gate_ready()
        loop(groups, chain_gate)

    def before_last():
        pl.when(place > 0)(lambda: loop(chunks, lambda c: chain(FWD, c)))
        pl.when(place < last - 1)(pull_ready)
        pull(jnp.where(place == last - 1, groups, 0), tiles)
        gate_ready()
        loop(groups, gate)

    pl.when(place == last)(at_last)
    pl.when(place < last)(before_last)

    lane = lax.broadcasted_iota(jnp.int32, (rows, 128), 1)
    stats = jnp.zeros((rows, 128), F32)
    for blk in (0, 1):
        for k in (0, 1):
            col = jnp.sum(r.sums[blk, k], axis=1, keepdims=True)
            stats = jnp.where(lane == 2 * blk + k, col, stats)
    r.stat_tx[...] = stats.T[0:8, :]
    st_copies = []
    for k, peer in enumerate(stat_peers):
        st_copies.append(remote(r.stat_tx, r.stat_rx.at[k], r.st_send, r.st_recv.at[k], peer))
        st_copies[-1].start()
    pl.when(place < last - 1)(lambda: send_n().start())
    total = r.stat_tx[...]
    for k, copy in enumerate(st_copies):
        copy.wait_recv()
        total = total + r.stat_rx[k]
    stat_cols = jnp.concatenate([total, jnp.zeros((rows - 8, rows), F32)], axis=0).T
    inv, back = [], []
    for blk in (0, 1):
        inv.append(lax.rsqrt(stat_cols[:, 2 * blk : 2 * blk + 1] / total_width + NORM_EPS))
        back.append(inv[blk] * inv[blk] * inv[blk] * stat_cols[:, 2 * blk + 1 : 2 * blk + 2] / total_width)
        r.invs[blk] = jnp.broadcast_to(inv[blk], (rows, 128))
        r.backs[blk] = jnp.broadcast_to(back[blk], (rows, 128))

    def wide(ref, blk):
        return jnp.concatenate([ref[blk]] * (gw // 128), axis=1)

    def cotangent(g):
        cols = gcols(g)
        for blk in (0, 1):
            gated = r.gated[blk, :, cols]
            d_normed = wide(r.invs, blk) * r.pv[blk, g].astype(F32)
            d = ((gain_of(g) * d_normed - wide(r.backs, blk) * gated) * r.act[blk, :, cols]).astype(BF16)
            r.d[blk, :, cols] = d
            weighted = (r.carry_e[blk, :, cols] * d.astype(F32)).astype(BF16)
            block = dot(r.ct[blk], weighted)
            for k in range(group):
                r.f[blk, g * group + k] = block[:, k * cw : (k + 1) * cw]

    def cotangent_chain(g):
        cotangent(g)
        chain_group(BWD, g)

    pl.when(place == last)(lambda: loop(groups, cotangent_chain))
    pl.when(place < last)(lambda: loop(groups, cotangent))

    def terms(g):
        cols = gcols(g)
        gain_sum = skip_sum = None
        for blk in (0, 1):
            a = r.gated[blk, :, cols] * (wide(r.invs, blk) * r.pv[blk, g].astype(F32))
            s = r.d[blk, :, cols].astype(F32) * x_group(blk, g)
            gain_sum = a if gain_sum is None else gain_sum + a
            skip_sum = s if skip_sum is None else skip_sum + s
        r.red_tx[0, 0:1, cols] = jnp.sum(gain_sum, axis=0, keepdims=True)
        r.red_tx[0, 1:2, cols] = jnp.sum(skip_sum, axis=0, keepdims=True)

    loop(groups, terms)

    root = n_dp - 1

    def red_root(k):
        to = {"dp": root}
        return remote(r.red_tx.at[0], r.red_rx.at[k], r.rd_send.at[0], r.rd_recv.at[k], to)

    everyone = [
        {"seq": lax.rem(seq + k, n_seq), "dp": lax.rem(dp + j, n_dp)}
        for k in range(n_seq)
        for j in range(n_dp)
        if (k, j) != (0, 0)
    ]

    def red_all(which, k):
        return remote(r.red_tx.at[1], r.fin.at[which], r.fin_send, r.fin_recv, everyone[k])

    for k in range(root):
        pl.when(dp == k)(red_root(k).start)

    def spread_sums():
        total = r.red_tx[0]
        for k in range(root):
            red_root(k).wait_recv()
            total = total + r.red_rx[k]
        r.red_tx[1] = total
        r.fin[seq] = total
        for k in range(len(everyone)):
            red_all(seq, k).start()


    def intra_back(blk):
        for q in range(hh // 2):
            cols = slice(q * 2 * hd, (q + 1) * 2 * hd)
            two = r.d[blk, :, cols]
            r.inside[blk, :, cols] = dot_rows(r.mix[blk, q], block_diag(two)) + r.skip_e[:, cols] * two.astype(
                F32
            )

    intra_back(other)
    intra_back(mine)
    pl.when(late_place)(lambda: send_n().start())
    pl.when(place == 0)(relay)
    pl.when(dp == root)(spread_sums)

    tile_n = min(256, nb)
    per = nb // tile_n
    sent_tiles = (n_chan - 1) * per

    def pj(t):
        to = {"chan": lax.rem(chan + 1 + t // per, n_chan)}
        return remote(r.proj_tx.at[t], r.proj_rx.at[t], r.pj_send, r.pj_recv.at[t], to)

    def project(t):
        block = lax.rem(chan + 1 + t // per, n_chan)
        at = pl.ds(pl.multiple_of(block * nb + lax.rem(t, per) * tile_n, tile_n), tile_n)
        value = dot(r.nrm[mine], r.wv[my_half, at]) + dot(r.nrx[...], r.wv[other_half, at])

        @pl.when(t < sent_tiles)
        def _():
            r.proj_tx[t] = value.astype(BF16)
            pj(t).start()

        @pl.when(t >= sent_tiles)
        def _():
            r.proj_own[t - sent_tiles] = value

    n_tiles = sent_tiles + per

    def finish(c):
        cols = ccols(c)

        def value(blk):
            carried = dot(r.bv[blk], r.st[BWD, blk, c])
            return (r.inside[blk, :, cols] + r.tdt_e[blk, :, cols] * carried).astype(BF16)

        r.gtx[c] = value(other)
        send_g(c, mine).start()
        r.gx[:, pl.ds(pl.multiple_of(mine * half + c * cw, cw), cw)] = value(mine)

    def chain_finish(c):
        chain(BWD, c)
        finish(c)

    def back_first():
        send_n().wait_recv()
        loop(sent_tiles, project)
        loop(chunks, chain_finish)
        loop(per, lambda t: project(sent_tiles + t))

    def back_middle():
        loop(chunks, lambda c: chain(BWD, c))
        loop(chunks, finish)
        send_n().wait_recv()
        loop(n_tiles, project)

    def back_last():
        loop(chunks, finish)
        send_n().wait_recv()
        loop(n_tiles, project)

    pl.when(place == 0)(back_first)
    pl.when((place > 0) & (place < last))(back_middle)
    pl.when(place == last)(back_last)
    inv_mine = jnp.concatenate([r.invs[mine]] * (tile_n // 128), axis=1)
    for i in range(per):
        value = r.proj_own[i]
        for k in range(n_chan - 1):
            pj(k * per + i).wait_recv()
            value = value + r.proj_rx[k * per + i].astype(F32)
        r.out[:, i * tile_n : (i + 1) * tile_n] = (inv_mine * value).astype(BF16)

    def all_sent(ref, sem):
        remote(ref, ref, sem, r.fin_recv, partner).wait_send()

    def sums_arrive(n):
        remote(r.fin.at[0:n], r.fin.at[0:n], r.fin_send, r.fin_recv, partner).wait_recv()

    pl.when(dp < root)(lambda: sums_arrive(n_seq))
    pl.when(dp == root)(lambda: sums_arrive(n_seq - 1))
    skip_total = jnp.zeros((8, heads), F32)
    for which in (0, 1):
        final = r.fin[which]
        for k in range(1, n_seq // 2):
            final = final + r.fin[2 * k + which]
        r.gg[:, which * half : (which + 1) * half] = final[0:1, :]
        skip_cols = jnp.concatenate([final[1:2, :], jnp.zeros((7, half), F32)], axis=0)
        for part in split(skip_cols, 3):
            skip_total = skip_total + dot_cols(part, spread_all(which))
    r.gs[...] = skip_total[0:1, :]

    for c in range(chunks):
        send_g(c, other).wait_recv()

    for copy in [send_sm(mine), send_b(mine), send_c(mine), send_z(mine), send_n()]:
        copy.wait_send()
    for copy in do_copies:
        copy.wait_send()
    all_sent(r.stat_rx, r.st_send)
    if sent_tiles:
        all_sent(r.proj_tx, r.pj_send)
    all_sent(r.xo, r.x_send)
    all_sent(r.gtx, r.g_send)
    all_sent(r.ptx, r.pl_send)
    for k in range(root):
        pl.when(dp == k)(red_root(k).wait_send)
    pl.when(dp == root)(lambda: all_sent(r.fin.at[0 : n_seq * n_dp - 1], r.fin_send))
    pl.when(has_prev)(lambda: all_sent(r.txc.at[BWD], r.c_send.at[BWD]))
    pl.when(has_next)(lambda: all_sent(r.txc.at[FWD], r.c_send.at[FWD]))


def hand_over(*refs):
    for source, target in zip(refs[:4], refs[4:]):
        target[...] = source[...]


def local(
    mesh_shape, ssm_input, gate_z, b_proj, c_proj, step_size, log_decay, skip_d, norm_gain, w_out, d_out, game_lengths
):
    n_seq, n_chan, n_dp = (mesh_shape[a] for a in ("seq", "chan", "dp"))
    _, rows, width = ssm_input.shape
    heads = step_size.shape[2]
    states = b_proj.shape[2]
    model = w_out.shape[1]
    nb = d_out.shape[2]
    half = width // 2
    hh = heads // 2
    chunks = max(1, min(8, half // 128))
    cw = half // chunks
    group = 2 if chunks % 2 == 0 else 1
    gw = group * cw
    groups = chunks // group
    peers = max(1, n_chan - 1)
    tile_n = min(256, nb)
    tiles = peers * (nb // tile_n)
    stat_peers = 2 * n_chan - 1
    games = game_lengths.shape[1]
    sizes = (n_seq, n_chan, n_dp, heads, games, chunks, group)
    vmem = pl.BlockSpec(memory_space=pltpu.VMEM)
    hbm = pl.BlockSpec(memory_space=pltpu.HBM)

    def dma(*shape):
        return pltpu.SemaphoreType.DMA(shape)

    inputs = dict(
        x=ssm_input[0],
        b=b_proj[0],
        c=c_proj[0],
        dt=step_size[0].T,
        ld=log_decay[0].T,
        skip=skip_d[None],
        gain=norm_gain[None],
        gl=game_lengths,
        z=gate_z[0],
        w=w_out,
        do=d_out[0],
    )
    outputs = dict(
        out=pltpu.VMEM((rows, nb), BF16),
        gx=pltpu.VMEM((rows, width), BF16),
        gg=pltpu.VMEM((1, width), F32),
        gs=pltpu.VMEM((1, heads), F32),
    )
    both = (2, rows, half)
    scratch = dict(
        xv=pltpu.VMEM((2, chunks, rows, cw), BF16),
        xo=pltpu.VMEM((chunks, rows, cw), BF16),
        zv=pltpu.VMEM(both, BF16),
        zo=pltpu.VMEM((rows, half), BF16),
        bv=pltpu.VMEM((2, rows, states), BF16),
        cv=pltpu.VMEM((2, rows, states), BF16),
        bt=pltpu.VMEM((2, states, rows), BF16),
        ct=pltpu.VMEM((2, states, rows), BF16),
        ldv=pltpu.VMEM((heads, rows), F32),
        smf=pltpu.VMEM((2, heads, rows), F32),
        sm=pltpu.VMEM((2, 2, hh, rows), F32),
        runc=pltpu.VMEM((2, rows, hh), F32),
        skipv=pltpu.VMEM((1, heads), F32),
        gainv=pltpu.VMEM((1, width), F32),
        gls=pltpu.SMEM((1, games), jnp.int32),
        wv=pltpu.VMEM((width, model), BF16),
        dfull=pltpu.VMEM((n_chan, rows, nb), BF16),
        carry_e=pltpu.VMEM(both, F32),
        tdt_e=pltpu.VMEM(both, F32),
        skip_e=pltpu.VMEM((1, half), F32),
        mix=pltpu.VMEM((2, hh // 2, 2 * rows, rows), BF16),
        inside=pltpu.VMEM(both, F32),
        act=pltpu.VMEM(both, F32),
        gated=pltpu.VMEM(both, F32),
        nrm=pltpu.VMEM(both, BF16),
        nrx=pltpu.VMEM((rows, half), BF16),
        d=pltpu.VMEM(both, BF16),
        ptx=pltpu.VMEM((groups, rows, gw), BF16),
        pv=pltpu.VMEM((2, groups, rows, gw), BF16),
        f=pltpu.VMEM((2, chunks, states, cw), F32),
        txc=pltpu.VMEM((2, chunks, states, cw), BF16),
        st=pltpu.VMEM((2, 2, chunks, states, cw), BF16),
        sums=pltpu.VMEM((2, 2, rows, 128), F32),
        invs=pltpu.VMEM((2, rows, 128), F32),
        backs=pltpu.VMEM((2, rows, 128), F32),
        stat_tx=pltpu.VMEM((8, rows), F32),
        stat_rx=pltpu.VMEM((stat_peers, 8, rows), F32),
        proj_tx=pltpu.VMEM((tiles, rows, tile_n), BF16),
        proj_rx=pltpu.VMEM((tiles, rows, tile_n), BF16),
        proj_own=pltpu.VMEM((nb // tile_n, rows, tile_n), F32),
        gtx=pltpu.VMEM((chunks, rows, cw), BF16),
        red_tx=pltpu.VMEM((2, 2, half), F32),
        red_rx=pltpu.VMEM((max(1, n_dp - 1), 2, half), F32),
        fin=pltpu.VMEM((n_seq * n_dp, 2, half), F32),
        load_sem=dma(13),
        p_send=dma(5),
        p_recv=dma(5),
        x_send=pltpu.SemaphoreType.DMA,
        x_recv=dma(chunks),
        pl_send=pltpu.SemaphoreType.DMA,
        pl_recv=dma(groups),
        g_send=pltpu.SemaphoreType.DMA,
        g_recv=dma(chunks),
        c_send=dma(2),
        c_recv=dma(2, chunks),
        do_send=dma(peers),
        do_recv=dma(peers),
        st_send=pltpu.SemaphoreType.DMA,
        st_recv=dma(stat_peers),
        pj_send=pltpu.SemaphoreType.DMA,
        pj_recv=dma(tiles),
        rd_send=dma(1),
        rd_recv=dma(max(1, n_dp - 1)),
        fin_send=pltpu.SemaphoreType.DMA,
        fin_recv=pltpu.SemaphoreType.DMA,
        go=pltpu.SemaphoreType.REGULAR,
        up=pltpu.SemaphoreType.REGULAR,
    )
    names = tuple(inputs) + tuple(outputs) + tuple(scratch)
    results = pl.pallas_call(
        functools.partial(kernel, sizes, names),
        out_shape=tuple(outputs.values()),
        in_specs=[hbm] * len(inputs),
        out_specs=(vmem,) * 4,
        scratch_shapes=list(scratch.values()),
        compiler_params=pltpu.CompilerParams(
            collective_id=0, has_side_effects=True, vmem_limit_bytes=60 * 1024 * 1024
        ),
    )(*inputs.values())
    out, gx, gg, gs = pl.pallas_call(
        hand_over,
        out_shape=tuple(jax.ShapeDtypeStruct(a.shape, a.dtype) for a in results),
        in_specs=[vmem] * 4,
        out_specs=(vmem,) * 4,
        compiler_params=pltpu.CompilerParams(vmem_limit_bytes=4 * 1024 * 1024),
    )(*results)
    return out[None], gx[None], gg[0], gs[0]


def solution(mesh):
    return jax.shard_map(
        functools.partial(local, dict(mesh.shape)),
        mesh=mesh,
        in_specs=(
            P("dp", "seq", "chan"),
            P("dp", "seq", "chan"),
            P("dp", "seq", None),
            P("dp", "seq", None),
            P("dp", "seq", "chan"),
            P("dp", "seq", "chan"),
            P("chan"),
            P("chan"),
            P("chan", None),
            P("dp", "seq", "chan"),
            P("dp", None),
        ),
        out_specs=(P("dp", "seq", "chan"), P("dp", "seq", "chan"), P("chan"), P("chan")),
        check_vma=False,
    )
```

time: 50.6 us -> 45.4 us (0.90)
  the two profiles are of different devices: /device:TPU:0 before, /device:TPU:1 now
where the time goes in v1:
time: 45.4 us; the launch traced here: 45.2 us
  Pallas kernels  44.5 us (98%)
  between operations  0.64 us (1%)
    pallas_call x1, Pallas kernels, local(): pl.pallas_call(functools.partial(kernel, sizes, names), out_shape=tuple(o...  43.6 us
    pallas_call x1, Pallas kernels, local(): pl.pallas_call(hand_over, out_shape=tuple((jax.ShapeDtypeStruct(a.shape,...  0.93 us

profile of v1, /device:TPU:1, one launch (start us, length us, event | category | flops | bytes accessed | tf_op | source)
XLA Modules:
  0.0 45.2 jit_solution(15506456372429018294)
XLA Ops:
  0.6 43.6 %shard_map.138 = (bf16[128,1024]{1,0:T(8,128)(2,1)S(1)}, bf16[128,2048]{1,0:T(8,128)(2,1)S(1)}, f32[1,2048]{1,0:T(1,128)S(1)}, f32[1,32]{1,0:T(1,128)S(1)}) custom-call(bf16[128,2048]{1,0:T(8,128)(2,1)} %bitcast.17, bf16[128,128]{1,0:T(8,128)(2,1)} %bitcast.20, bf16[128,128]{1,0:T(8,128)(2,1)} %bitcast.21, f32[32,128]{1,0:T(8,128)} %bitcast.22, ...), custom_call_target="tpu_custom_call" | custom-call | tf_op jit(solution)/shard_map/pallas_call | solution.py:794
  44.2 0.9 %shard_map.139 = (bf16[128,1024]{1,0:T(8,128)(2,1)}, bf16[128,2048]{1,0:T(8,128)(2,1)}, f32[1,2048]{1,0:T(1,128)}, f32[1,32]{1,0:T(1,128)}) custom-call(bf16[128,1024]{1,0:T(8,128)(2,1)S(1)} %get-tuple-element.12.refs_0_, bf16[128,2048]{1,0:T(8,128)(2,1)S(1)} %get-tuple-element.13.refs_1_, f32[1,2048]{1,0:T(1,128)S(1)} %get-tuple-element.14.refs_2_, ...), custom_call_target="tpu_custom_call" | custom-call | tf_op jit(solution)/shard_map/pallas_call | solution.py:804

commit v2 on v1

--- a/solution.py
+++ b/solution.py
@@ -85,9 +85,9 @@
         order[name].start()
 
     def load_chunks(name, which, dst):
-        for c in range(chunks):
-            at = pl.ds(pl.multiple_of(which * half + c * cw, cw), cw)
-            pltpu.make_async_copy(r.x.at[:, at], dst.at[c], r.load_sem.at[len(order)]).start()
+        for g in range(groups):
+            at = pl.ds(pl.multiple_of(which * half + g * gw, gw), gw)
+            pltpu.make_async_copy(r.x.at[:, at], dst.at[g], r.load_sem.at[len(order)]).start()
         order[name] = pltpu.make_async_copy(dst, dst, r.load_sem.at[len(order)])
 
     load("ld", r.ld, r.ldv)
@@ -134,19 +134,32 @@
     def send_n():
         return remote(r.nrm.at[other], r.nrx, r.p_send.at[4], r.p_recv.at[4], partner)
 
-    def send_x(blk, c):
-        return remote(r.xo.at[c], r.xv.at[blk, c], r.x_send, r.x_recv.at[c], partner)
+    def send_x(blk, g):
+        return remote(r.xo.at[g], r.xv.at[blk, g], r.x_send, r.x_recv.at[g], partner)
 
     def send_p(blk, g):
         return remote(r.ptx.at[g], r.pv.at[blk, g], r.pl_send, r.pl_recv.at[g], partner)
 
-    def send_g(c, of):
-        at = pl.ds(pl.multiple_of(of * half + c * cw, cw), cw)
-        return remote(r.gtx.at[c], r.gx.at[:, at], r.g_send, r.g_recv.at[c], partner)
-
-    def send_chain(d, c):
-        to = next_dev if d == FWD else prev_dev
-        return remote(r.txc.at[d, c], r.st.at[d, d, c], r.c_send.at[d], r.c_recv.at[d, c], to)
+    def send_g(g, of):
+        at = pl.ds(pl.multiple_of(of * half + g * gw, gw), gw)
+        return remote(r.gtx.at[g], r.gx.at[:, at], r.g_send, r.g_recv, partner)
+
+    half_way = n_seq // 4 - 1 if n_seq >= 4 else 0
+    spots = (place, last - place)
+    early = (dp == 0, dp == n_dp - 1)
+    plain_end = tuple(last - e.astype(jnp.int32) for e in early)
+
+    def onward(d):
+        return next_dev if d == FWD else prev_dev
+
+    def send_late(d, c):
+        return remote(r.txc.at[d, c], r.st.at[d, d, c], r.c_send.at[d], r.c_recv.at[d, c], onward(d))
+
+    def send_early(d, c):
+        return remote(r.txe.at[d, c], r.ex.at[d, c], r.e_send.at[d], r.e_recv.at[d, c], onward(d))
+
+    def send_final(d, c):
+        return remote(r.txe.at[d, c], r.st.at[d, d, c], r.e_send.at[d], r.c_recv.at[d, c], onward(d))
 
     do_copies = [
         remote(r.dfull.at[0], r.dfull.at[k + 1], r.do_send.at[k], r.do_recv.at[k], peer)
@@ -208,12 +221,13 @@
 
     my_heads = pl.ds(pl.multiple_of(mine * hh, hh), hh)
     order["dt"].wait()
-    r.sm[mine] = r.smf[:, my_heads, :]
     order["b"].wait()
-    prepare(mine)
 
     def report():
         pl.semaphore_signal(r.up, inc=1, device_id=prev_dev, device_id_type=MESH)
+
+    def report_up():
+        pl.semaphore_signal(r.up, inc=1, device_id=next_dev, device_id_type=MESH)
 
     def relay():
         pl.semaphore_wait(r.up, 1)
@@ -230,8 +244,8 @@
     def first_sends():
         send_sm(mine).start()
         send_b(mine).start()
-        for c in range(chunks):
-            send_x(mine, c).start()
+        for g in range(groups):
+            send_x(mine, g).start()
         send_c(mine).start()
 
     def cotangent_sends():
@@ -247,10 +261,12 @@
 
     pl.when(dp == 0)(lead_sends)
     pl.when((dp == 0) & (place >= last - 1))(gate_sends)
+    r.sm[mine] = r.smf[:, my_heads, :]
+    prepare(mine)
     order["x"].wait()
 
     def x_group(blk, g):
-        return jnp.concatenate([r.xv[blk, g * group + k] for k in range(group)], axis=1).astype(F32)
+        return r.xv[blk, g].astype(F32)
 
 
     def fresh(blk, g):
@@ -295,7 +311,7 @@
                 mixes.append((jnp.exp(gap) * scores * r.sm[blk, 1, h : h + 1, :]).astype(BF16))
                 r.mix[blk, q, (h % 2) * rows : (h % 2 + 1) * rows, :] = mixes[-1]
             at = q * 2 * hd
-            two = r.xv[blk, at // cw, :, at % cw : at % cw + 2 * hd]
+            two = r.xv[blk, at // gw, :, at % gw : at % gw + 2 * hd]
             r.inside[blk, :, cols] = dot(jnp.concatenate(mixes, axis=1), block_diag(two)) + r.skip_e[
                 :, cols
             ] * two.astype(F32)
@@ -307,30 +323,57 @@
 
         loop(groups, body)
 
+    def dims(d):
+        return (0, 1) if d == FWD else (1, 0)
+
+    def through(d, c, mid):
+        two = dims(d)[1]
+        return (r.carry_e[two, rows - 1 : rows, ccols(c)] * mid + r.f[two, c]).astype(BF16)
+
+    def enter(d, c, state):
+        one = dims(d)[0]
+        return r.carry_e[one, rows - 1 : rows, ccols(c)] * state.astype(F32) + r.f[one, c]
+
     def chain(d, c):
-        enters = has_prev if d == FWD else has_next
-        leaves = has_next if d == FWD else has_prev
-
-        @pl.when(enters)
+        spot = spots[d]
+
+        @pl.when(spot > 0)
         def _():
-            send_chain(d, c).wait_recv()
-
-        @pl.when(jnp.logical_not(enters))
+            send_late(d, c).wait_recv()
+
+        @pl.when(spot == 0)
         def _():
             r.st[d, d, c] = jnp.zeros((r.st.shape[3], cw), BF16)
 
-        one, two = (0, 1) if d == FWD else (1, 0)
-        mid = r.carry_e[one, rows - 1 : rows, ccols(c)] * r.st[d, d, c].astype(F32) + r.f[one, c]
+        mid = enter(d, c, r.st[d, d, c])
         r.st[d, 1 - d, c] = mid.astype(BF16)
 
-        @pl.when(leaves)
+        @pl.when(spot < plain_end[d])
         def _():
-            r.txc[d, c] = (r.carry_e[two, rows - 1 : rows, ccols(c)] * mid + r.f[two, c]).astype(BF16)
-            send_chain(d, c).start()
+            r.txc[d, c] = through(d, c, mid)
+            send_late(d, c).start()
+
+    def early_start(d, c):
+        spot = spots[d]
+        r.txe[d, c] = through(d, c, r.f[dims(d)[0], c])
+        pl.when(spot == last - 1)(send_final(d, c).start)
+        pl.when(spot < last - 1)(send_early(d, c).start)
+
+    def early_pass(d, c):
+        spot = spots[d]
+        send_early(d, c).wait_recv()
+        r.txe[d, c] = through(d, c, enter(d, c, r.ex[d, c]))
+        pl.when(spot == last - 1)(send_final(d, c).start)
+        pl.when(spot < last - 1)(send_early(d, c).start)
+
+    def starts_early(d):
+        return early[d] & (spots[d] == half_way) & (spots[d] < last)
+
+    def passes_early(d):
+        return early[d] & (spots[d] > half_way) & (spots[d] < last)
 
     def meet(g):
-        for k in range(group):
-            send_x(other, g * group + k).wait_recv()
+        send_x(other, g).wait_recv()
         fresh(other, g)
 
     def partner_arrives():
@@ -344,6 +387,14 @@
     def meet_chain(g):
         meet(g)
         chain_group(FWD, g)
+
+    def early_group(d, g):
+        for k in range(group):
+            early_start(d, g * group + k)
+
+    def meet_early(g):
+        meet(g)
+        early_group(FWD, g)
 
     def own_local():
         intra(mine)
@@ -352,6 +403,7 @@
 
     def late_sends():
         own_local()
+        pl.when(place == last - 1)(relay)
         pl.semaphore_wait(r.go, 1)
         lead_sends()
         pl.when(place >= last - 1)(gate_sends)
@@ -364,7 +416,7 @@
     partner_arrives()
     pl.when((dp == 0) & (place < last - 1))(lead_done)
     prepare(other)
-    pl.when(place == last - 1)(relay)
+    pl.when((dp == 0) & (place == last - 1))(relay)
 
     def pull(lo, hi):
         def body(i, _):
@@ -407,12 +459,15 @@
 
     pl.when(late_place)(pull_first)
     pl.when(place == 0)(lambda: loop(groups, meet_chain))
-    pl.when(place > 0)(lambda: loop(groups, meet))
+    pl.when((place > 0) & starts_early(FWD))(lambda: loop(groups, meet_early))
+    pl.when((place == 0) & starts_early(FWD))(lambda: loop(groups, lambda g: early_group(FWD, g)))
+    pl.when((place > 0) & jnp.logical_not(starts_early(FWD)))(lambda: loop(groups, meet))
     pl.when((place > 0) & (place < last - 1))(relay)
+    pl.when((dp == 0) & (place < last - 1))(gate_sends)
     pl.when((dp == 0) & (place < last - 1))(own_local)
     send_c(other).wait_recv()
     intra(other)
-    pl.when(place < last - 1)(gate_sends)
+    pl.when((dp > 0) & (place < last - 1))(gate_sends)
     pl.when(place == last)(lambda: pull(groups, tiles))
     order["gain"].wait()
     r.sums[...] = jnp.zeros(r.sums.shape, F32)
@@ -449,10 +504,20 @@
         gate_ready()
         loop(groups, chain_gate)
 
-    def before_last():
-        pl.when(place > 0)(lambda: loop(chunks, lambda c: chain(FWD, c)))
+    def pull_rest():
         pl.when(place < last - 1)(pull_ready)
         pull(jnp.where(place == last - 1, groups, 0), tiles)
+
+    def pass_and_pull():
+        loop(chunks, lambda c: early_pass(FWD, c))
+        pull_rest()
+
+    def before_last():
+        passes = passes_early(FWD)
+        pl.when(passes)(pass_and_pull)
+        pl.when(place > 0)(lambda: loop(chunks, lambda c: chain(FWD, c)))
+        pl.when(place == last - 1)(report_up)
+        pl.when(jnp.logical_not(passes))(pull_rest)
         gate_ready()
         loop(groups, gate)
 
@@ -468,12 +533,13 @@
     r.stat_tx[...] = stats.T[0:8, :]
     st_copies = []
     for k, peer in enumerate(stat_peers):
-        st_copies.append(remote(r.stat_tx, r.stat_rx.at[k], r.st_send, r.st_recv.at[k], peer))
+        st_copies.append(remote(r.stat_tx, r.stat_rx.at[k], r.st_send, r.st_recv, peer))
         st_copies[-1].start()
-    pl.when(place < last - 1)(lambda: send_n().start())
+    lags = (dp == 0) & late_place
+    pl.when(jnp.logical_not(lags))(lambda: send_n().start())
     total = r.stat_tx[...]
-    for k, copy in enumerate(st_copies):
-        copy.wait_recv()
+    remote(r.stat_rx, r.stat_rx, r.st_send, r.st_recv, partner).wait_recv()
+    for k in range(len(stat_peers)):
         total = total + r.stat_rx[k]
     stat_cols = jnp.concatenate([total, jnp.zeros((rows - 8, rows), F32)], axis=0).T
     inv, back = [], []
@@ -502,8 +568,17 @@
         cotangent(g)
         chain_group(BWD, g)
 
+    def cotangent_early(g):
+        cotangent(g)
+        early_group(BWD, g)
+
+    begins = starts_early(BWD)
     pl.when(place == last)(lambda: loop(groups, cotangent_chain))
-    pl.when(place < last)(lambda: loop(groups, cotangent))
+    pl.when((place < last) & begins)(lambda: loop(groups, cotangent_early))
+    pl.when((place == last) & begins)(lambda: loop(groups, lambda g: early_group(BWD, g)))
+    pl.when((place < last) & jnp.logical_not(begins))(lambda: loop(groups, cotangent))
+
+    pl.when(lags)(lambda: send_n().start())
 
     def terms(g):
         cols = gcols(g)
@@ -524,15 +599,17 @@
         to = {"dp": root}
         return remote(r.red_tx.at[0], r.red_rx.at[k], r.rd_send.at[0], r.rd_recv.at[k], to)
 
-    everyone = [
-        {"seq": lax.rem(seq + k, n_seq), "dp": lax.rem(dp + j, n_dp)}
-        for k in range(n_seq)
-        for j in range(n_dp)
-        if (k, j) != (0, 0)
+    n_place = n_seq // 2
+    along = [{"seq": lax.rem(seq + 2 * k, n_seq)} for k in range(1, n_place)]
+    around = [
+        {"seq": seq if k == 0 else pair, "dp": lax.rem(dp + j, n_dp)} for k in (0, 1) for j in range(n_dp) if k or j
     ]
 
-    def red_all(which, k):
-        return remote(r.red_tx.at[1], r.fin.at[which], r.fin_send, r.fin_recv, everyone[k])
+    def red_along(where, k):
+        return remote(r.red_tx.at[1], r.red_z.at[where], r.fin_send.at[0], r.fin_recv.at[0], along[k])
+
+    def red_around(which, k):
+        return remote(r.fin.at[which], r.fin.at[which], r.fin_send.at[1], r.fin_recv.at[1 + which], around[k])
 
     for k in range(root):
         pl.when(dp == k)(red_root(k).start)
@@ -543,10 +620,19 @@
             red_root(k).wait_recv()
             total = total + r.red_rx[k]
         r.red_tx[1] = total
-        r.fin[seq] = total
-        for k in range(len(everyone)):
-            red_all(seq, k).start()
-
+        r.red_z[place] = total
+        for k in range(len(along)):
+            red_along(place, k).start()
+
+    def share_sums():
+        got = r.red_z.at[0 : n_place - 1]
+        remote(got, got, r.fin_send.at[0], r.fin_recv.at[0], partner).wait_recv()
+        total = r.red_z[0]
+        for k in range(1, n_place):
+            total = total + r.red_z[k]
+        r.fin[mine] = total
+        for k in range(len(around)):
+            red_around(mine, k).start()
 
     def intra_back(blk):
         for q in range(hh // 2):
@@ -558,8 +644,8 @@
 
     intra_back(other)
     intra_back(mine)
-    pl.when(late_place)(lambda: send_n().start())
     pl.when(place == 0)(relay)
+    pl.when(place == last)(lambda: pl.semaphore_wait(r.up, 1))
     pl.when(dp == root)(spread_sums)
 
     tile_n = min(256, nb)
@@ -586,36 +672,51 @@
 
     n_tiles = sent_tiles + per
 
-    def finish(c):
-        cols = ccols(c)
+    def finish(g):
+        cols = gcols(g)
 
         def value(blk):
-            carried = dot(r.bv[blk], r.st[BWD, blk, c])
+            carried = jnp.concatenate([dot(r.bv[blk], r.st[BWD, blk, g * group + k]) for k in range(group)], axis=1)
             return (r.inside[blk, :, cols] + r.tdt_e[blk, :, cols] * carried).astype(BF16)
 
-        r.gtx[c] = value(other)
-        send_g(c, mine).start()
-        r.gx[:, pl.ds(pl.multiple_of(mine * half + c * cw, cw), cw)] = value(mine)
-
-    def chain_finish(c):
-        chain(BWD, c)
-        finish(c)
+        theirs, ours = value(other), value(mine)
+        r.gtx[g] = theirs
+        send_g(g, mine).start()
+        r.gx[:, pl.ds(pl.multiple_of(mine * half + g * gw, gw), gw)] = ours
+
+    def chain_finish(g):
+        chain_group(BWD, g)
+        finish(g)
 
     def back_first():
         send_n().wait_recv()
         loop(sent_tiles, project)
-        loop(chunks, chain_finish)
+        chain_finish(0)
+        pl.when(dp == root)(share_sums)
+        loop(groups - 1, lambda g: chain_finish(1 + g))
         loop(per, lambda t: project(sent_tiles + t))
 
-    def back_middle():
-        loop(chunks, lambda c: chain(BWD, c))
-        loop(chunks, finish)
+    def project_all():
         send_n().wait_recv()
         loop(n_tiles, project)
 
+    def pass_and_project():
+        loop(chunks, lambda c: early_pass(BWD, c))
+        pl.when(dp == root)(share_sums)
+        project_all()
+
+    def back_middle():
+        passes = passes_early(BWD)
+        pl.when(passes)(pass_and_project)
+        loop(chunks, lambda c: chain(BWD, c))
+        loop(groups, finish)
+        pl.when((dp == root) & jnp.logical_not(passes))(share_sums)
+        pl.when(jnp.logical_not(passes))(project_all)
+
     def back_last():
-        loop(chunks, finish)
+        loop(groups, finish)
         send_n().wait_recv()
+        pl.when(dp == root)(share_sums)
         loop(n_tiles, project)
 
     pl.when(place == 0)(back_first)
@@ -630,26 +731,20 @@
         r.out[:, i * tile_n : (i + 1) * tile_n] = (inv_mine * value).astype(BF16)
 
     def all_sent(ref, sem):
-        remote(ref, ref, sem, r.fin_recv, partner).wait_send()
-
-    def sums_arrive(n):
-        remote(r.fin.at[0:n], r.fin.at[0:n], r.fin_send, r.fin_recv, partner).wait_recv()
-
-    pl.when(dp < root)(lambda: sums_arrive(n_seq))
-    pl.when(dp == root)(lambda: sums_arrive(n_seq - 1))
+        remote(ref, ref, sem, r.fin_recv.at[0], partner).wait_send()
+
+    red_around(other, 0).wait_recv()
+    pl.when(dp < root)(lambda: red_around(mine, 0).wait_recv())
     skip_total = jnp.zeros((8, heads), F32)
     for which in (0, 1):
         final = r.fin[which]
-        for k in range(1, n_seq // 2):
-            final = final + r.fin[2 * k + which]
         r.gg[:, which * half : (which + 1) * half] = final[0:1, :]
         skip_cols = jnp.concatenate([final[1:2, :], jnp.zeros((7, half), F32)], axis=0)
         for part in split(skip_cols, 3):
             skip_total = skip_total + dot_cols(part, spread_all(which))
     r.gs[...] = skip_total[0:1, :]
 
-    for c in range(chunks):
-        send_g(c, other).wait_recv()
+    remote(r.gtx, r.gtx, r.g_send, r.g_recv, partner).wait_recv()
 
     for copy in [send_sm(mine), send_b(mine), send_c(mine), send_z(mine), send_n()]:
         copy.wait_send()
@@ -663,14 +758,24 @@
     all_sent(r.ptx, r.pl_send)
     for k in range(root):
         pl.when(dp == k)(red_root(k).wait_send)
-    pl.when(dp == root)(lambda: all_sent(r.fin.at[0 : n_seq * n_dp - 1], r.fin_send))
-    pl.when(has_prev)(lambda: all_sent(r.txc.at[BWD], r.c_send.at[BWD]))
-    pl.when(has_next)(lambda: all_sent(r.txc.at[FWD], r.c_send.at[FWD]))
+
+    def sums_sent():
+        all_sent(r.red_z.at[0 : n_place - 1], r.fin_send.at[0])
+        all_sent(r.red_w, r.fin_send.at[1])
+
+    pl.when(dp == root)(sums_sent)
+    for d in (FWD, BWD):
+        pl.when(spots[d] < plain_end[d])(lambda d=d: all_sent(r.txc.at[d], r.c_send.at[d]))
+        pl.when(starts_early(d) | passes_early(d))(lambda d=d: all_sent(r.txe.at[d], r.e_send.at[d]))
 
 
 def hand_over(*refs):
-    for source, target in zip(refs[:4], refs[4:]):
-        target[...] = source[...]
+    sem = refs[8]
+    copies = [pltpu.make_async_copy(a, b, sem.at[k]) for k, (a, b) in enumerate(zip(refs[:4], refs[4:8]))]
+    for copy in copies:
+        copy.start()
+    for copy in copies:
+        copy.wait()
 
 
 def local(
@@ -722,8 +827,8 @@
     )
     both = (2, rows, half)
     scratch = dict(
-        xv=pltpu.VMEM((2, chunks, rows, cw), BF16),
-        xo=pltpu.VMEM((chunks, rows, cw), BF16),
+        xv=pltpu.VMEM((2, groups, rows, gw), BF16),
+        xo=pltpu.VMEM((groups, rows, gw), BF16),
         zv=pltpu.VMEM(both, BF16),
         zo=pltpu.VMEM((rows, half), BF16),
         bv=pltpu.VMEM((2, rows, states), BF16),
@@ -753,6 +858,8 @@
         pv=pltpu.VMEM((2, groups, rows, gw), BF16),
         f=pltpu.VMEM((2, chunks, states, cw), F32),
         txc=pltpu.VMEM((2, chunks, states, cw), BF16),
+        txe=pltpu.VMEM((2, chunks, states, cw), BF16),
+        ex=pltpu.VMEM((2, chunks, states, cw), BF16),
         st=pltpu.VMEM((2, 2, chunks, states, cw), BF16),
         sums=pltpu.VMEM((2, 2, rows, 128), F32),
         invs=pltpu.VMEM((2, rows, 128), F32),
@@ -762,31 +869,35 @@
         proj_tx=pltpu.VMEM((tiles, rows, tile_n), BF16),
         proj_rx=pltpu.VMEM((tiles, rows, tile_n), BF16),
         proj_own=pltpu.VMEM((nb // tile_n, rows, tile_n), F32),
-        gtx=pltpu.VMEM((chunks, rows, cw), BF16),
+        gtx=pltpu.VMEM((groups, rows, gw), BF16),
         red_tx=pltpu.VMEM((2, 2, half), F32),
         red_rx=pltpu.VMEM((max(1, n_dp - 1), 2, half), F32),
-        fin=pltpu.VMEM((n_seq * n_dp, 2, half), F32),
+        red_z=pltpu.VMEM((n_seq // 2, 2, half), F32),
+        red_w=pltpu.VMEM((2 * n_dp - 1, 2, half), F32),
+        fin=pltpu.VMEM((2, 2, half), F32),
         load_sem=dma(13),
         p_send=dma(5),
         p_recv=dma(5),
         x_send=pltpu.SemaphoreType.DMA,
-        x_recv=dma(chunks),
+        x_recv=dma(groups),
         pl_send=pltpu.SemaphoreType.DMA,
         pl_recv=dma(groups),
         g_send=pltpu.SemaphoreType.DMA,
-        g_recv=dma(chunks),
+        g_recv=pltpu.SemaphoreType.DMA,
         c_send=dma(2),
         c_recv=dma(2, chunks),
+        e_send=dma(2),
+        e_recv=dma(2, chunks),
         do_send=dma(peers),
         do_recv=dma(peers),
         st_send=pltpu.SemaphoreType.DMA,
-        st_recv=dma(stat_peers),
+        st_recv=pltpu.SemaphoreType.DMA,
         pj_send=pltpu.SemaphoreType.DMA,
         pj_recv=dma(tiles),
         rd_send=dma(1),
         rd_recv=dma(max(1, n_dp - 1)),
-        fin_send=pltpu.SemaphoreType.DMA,
-        fin_recv=pltpu.SemaphoreType.DMA,
+        fin_send=dma(2),
+        fin_recv=dma(3),
         go=pltpu.SemaphoreType.REGULAR,
         up=pltpu.SemaphoreType.REGULAR,
     )
@@ -805,7 +916,8 @@
         hand_over,
         out_shape=tuple(jax.ShapeDtypeStruct(a.shape, a.dtype) for a in results),
         in_specs=[vmem] * 4,
-        out_specs=(vmem,) * 4,
+        out_specs=(hbm,) * 4,
+        scratch_shapes=[dma(4)],
         compiler_params=pltpu.CompilerParams(vmem_limit_bytes=4 * 1024 * 1024),
     )(*results)
     return out[None], gx[None], gg[0], gs[0]

time: 45.4 us -> 43.9 us (0.967)
  Pallas kernels: 44.5 us -> 43.1 us
    pallas_call x1, Pallas kernels: 43.6 us -> 42.1 us  [local(): pl.pallas_call(functools.partial(kernel, sizes, names), out_shape=tuple(o...]
where the time goes in v2:
time: 43.9 us; the launch traced here: 43.7 us
  Pallas kernels  43.1 us (98%)
  between operations  0.64 us (1%)
    pallas_call x1, Pallas kernels, local(): pl.pallas_call(functools.partial(kernel, sizes, names), out_shape=tuple(o...  42.1 us
    pallas_call x1, Pallas kernels, local(): pl.pallas_call(hand_over, out_shape=tuple((jax.ShapeDtypeStruct(a.shape,...  0.92 us

profile of v2, /device:TPU:1, one launch (start us, length us, event | category | flops | bytes accessed | tf_op | source)
XLA Modules:
  0.0 43.7 jit_solution(12052444158907931435)
XLA Ops:
  0.6 42.1 %shard_map.138 = (bf16[128,1024]{1,0:T(8,128)(2,1)S(1)}, bf16[128,2048]{1,0:T(8,128)(2,1)S(1)}, f32[1,2048]{1,0:T(1,128)S(1)}, f32[1,32]{1,0:T(1,128)S(1)}) custom-call(bf16[128,2048]{1,0:T(8,128)(2,1)} %bitcast.17, bf16[128,128]{1,0:T(8,128)(2,1)} %bitcast.20, bf16[128,128]{1,0:T(8,128)(2,1)} %bitcast.21, f32[32,128]{1,0:T(8,128)} %bitcast.22, ...), custom_call_target="tpu_custom_call" | custom-call | tf_op jit(solution)/shard_map/pallas_call | solution.py:905
  42.8 0.9 %shard_map.139 = (bf16[128,1024]{1,0:T(8,128)(2,1)}, bf16[128,2048]{1,0:T(8,128)(2,1)}, f32[1,2048]{1,0:T(1,128)}, f32[1,32]{1,0:T(1,128)}) custom-call(bf16[128,1024]{1,0:T(8,128)(2,1)S(1)} %get-tuple-element.12.refs_0_, bf16[128,2048]{1,0:T(8,128)(2,1)S(1)} %get-tuple-element.13.refs_1_, f32[1,2048]{1,0:T(1,128)S(1)} %get-tuple-element.14.refs_2_, ...), custom_call_target="tpu_custom_call" | custom-call | tf_op jit(solution)/shard_map/pallas_call | solution.py:915

commit v3 on v2

--- a/solution.py
+++ b/solution.py
@@ -474,7 +474,6 @@
 
     def gate(g):
         cols = gcols(g)
-        send_p(other, g).wait_recv()
         for blk in (0, 1):
             carried = jnp.concatenate(
                 [dot(r.cv[blk], r.st[FWD, blk, g * group + k]) for k in range(group)], axis=1
@@ -484,12 +483,18 @@
             r.gated[blk, :, cols] = gated
             r.nrm[blk, :, cols] = normed
             sq = gated * gated
-            od = normed.astype(F32) * r.pv[blk, g].astype(F32)
-            squares, dots = r.sums[blk, 0], r.sums[blk, 1]
+            squares = r.sums[blk, 0]
             for k in range(gw // 128):
                 squares = squares + sq[:, k * 128 : (k + 1) * 128]
+            r.sums[blk, 0] = squares
+
+    def gate_dots(g):
+        send_p(other, g).wait_recv()
+        for blk in (0, 1):
+            od = r.nrm[blk, :, gcols(g)].astype(F32) * r.pv[blk, g].astype(F32)
+            dots = r.sums[blk, 1]
+            for k in range(gw // 128):
                 dots = dots + od[:, k * 128 : (k + 1) * 128]
-            r.sums[blk, 0] = squares
             r.sums[blk, 1] = dots
 
     def gate_ready():
@@ -503,6 +508,7 @@
     def at_last():
         gate_ready()
         loop(groups, chain_gate)
+        loop(groups, gate_dots)
 
     def pull_rest():
         pl.when(place < last - 1)(pull_ready)
@@ -520,6 +526,7 @@
         pl.when(jnp.logical_not(passes))(pull_rest)
         gate_ready()
         loop(groups, gate)
+        loop(groups, gate_dots)
 
     pl.when(place == last)(at_last)
     pl.when(place < last)(before_last)
@@ -684,6 +691,22 @@
         send_g(g, mine).start()
         r.gx[:, pl.ds(pl.multiple_of(mine * half + g * gw, gw), gw)] = ours
 
+    def finish_chunk(c):
+        cols = ccols(c)
+        g, k = c // group, c % group
+
+        def value(blk):
+            carried = dot(r.bv[blk], r.st[BWD, blk, c])
+            return (r.inside[blk, :, cols] + r.tdt_e[blk, :, cols] * carried).astype(BF16)
+
+        def at(of):
+            return pl.ds(pl.multiple_of(of * half + c * cw, cw), cw)
+
+        piece = r.gtx.at[g, :, k * cw : (k + 1) * cw]
+        r.gtx[g, :, k * cw : (k + 1) * cw] = value(other)
+        remote(piece, r.gx.at[:, at(mine)], r.g_send, r.g_recv, partner).start()
+        r.gx[:, at(mine)] = value(mine)
+
     def chain_finish(g):
         chain_group(BWD, g)
         finish(g)
@@ -693,7 +716,11 @@
         loop(sent_tiles, project)
         chain_finish(0)
         pl.when(dp == root)(share_sums)
-        loop(groups - 1, lambda g: chain_finish(1 + g))
+        loop(max(0, groups - 2), lambda g: chain_finish(1 + g))
+        if groups > 1:
+            for c in range(chunks - group, chunks):
+                chain(BWD, c)
+                finish_chunk(c)
         loop(per, lambda t: project(sent_tiles + t))
 
     def project_all():

time: 43.9 us -> 43.8 us (level)
  no operation moved by 1% of the time
where the time goes in v3:
time: 43.8 us; the launch traced here: 43.5 us
  Pallas kernels  42.8 us (98%)
  between operations  0.64 us (1%)
    pallas_call x1, Pallas kernels, local(): pl.pallas_call(functools.partial(kernel, sizes, names), out_shape=tuple(o...  41.9 us
    pallas_call x1, Pallas kernels, local(): pl.pallas_call(hand_over, out_shape=tuple((jax.ShapeDtypeStruct(a.shape,...  0.92 us

profile of v3, /device:TPU:1, one launch (start us, length us, event | category | flops | bytes accessed | tf_op | source)
XLA Modules:
  0.0 43.5 jit_solution(2176619175855947321)
XLA Ops:
  0.6 41.9 %shard_map.138 = (bf16[128,1024]{1,0:T(8,128)(2,1)S(1)}, bf16[128,2048]{1,0:T(8,128)(2,1)S(1)}, f32[1,2048]{1,0:T(1,128)S(1)}, f32[1,32]{1,0:T(1,128)S(1)}) custom-call(bf16[128,2048]{1,0:T(8,128)(2,1)} %bitcast.17, bf16[128,128]{1,0:T(8,128)(2,1)} %bitcast.20, bf16[128,128]{1,0:T(8,128)(2,1)} %bitcast.21, f32[32,128]{1,0:T(8,128)} %bitcast.22, ...), custom_call_target="tpu_custom_call" | custom-call | tf_op jit(solution)/shard_map/pallas_call | solution.py:932
  42.6 0.9 %shard_map.139 = (bf16[128,1024]{1,0:T(8,128)(2,1)}, bf16[128,2048]{1,0:T(8,128)(2,1)}, f32[1,2048]{1,0:T(1,128)}, f32[1,32]{1,0:T(1,128)}) custom-call(bf16[128,1024]{1,0:T(8,128)(2,1)S(1)} %get-tuple-element.12.refs_0_, bf16[128,2048]{1,0:T(8,128)(2,1)S(1)} %get-tuple-element.13.refs_1_, f32[1,2048]{1,0:T(1,128)S(1)} %get-tuple-element.14.refs_2_, ...), custom_call_target="tpu_custom_call" | custom-call | tf_op jit(solution)/shard_map/pallas_call | solution.py:942
